TPU v7x, 32 devices: a whole 2x2x4 slice. The times are simulated.
32 devices in a mesh: row: 2 (over x), col: 4 (over z), depth: 4 (over y, core).
Axes of the slice: x: 2, y: 2, z: 4, core: 2. Of those that a mesh axis runs over, the one named last changes fastest.
Arguments:
- acts: bfloat16 [8192, 5120], P(('depth', 'col'), 'row'), may hold values from -6 to 6
- grad_out: bfloat16 [8192, 13824], P(('depth', 'row'), 'col'), may hold values from -6 to 6
- weight: bfloat16 [5120, 13824], P('row', 'col'), may hold values from -0.078125 to 0.078125
- master: float32 [5120, 13824], P(('row', 'depth'), 'col'), may hold values from -0.078125 to 0.078125
- moment_one: float32 [5120, 13824], P(('row', 'depth'), 'col'), may hold values from -4 to 4
- moment_two: float32 [5120, 13824], P(('row', 'depth'), 'col'), may hold values from 0.05 to 2
Outputs:
- grad_in: bfloat16 [8192, 5120], P(('depth', 'col'), 'row')
- new_weight: bfloat16 [5120, 13824], P('row', 'col')
- new_master: float32 [5120, 13824], P(('row', 'depth'), 'col')
- new_moment_one: float32 [5120, 13824], P(('row', 'depth'), 'col')
- new_moment_two: float32 [5120, 13824], P(('row', 'depth'), 'col')
All inputs are finite; a program needn't handle non-finite values.
Results may differ from a plain program's by a relative error of at most 0.0035.
Values may be sent and summed in bfloat16 or wider, within the bound.
A program may use at most 192 MiB of HBM per device.

v0:
```python
import math
import jax
import jax.numpy as jnp
from jax import lax
from jax.sharding import PartitionSpec as P

STEP = 10


def per_device(acts, grad_out, weight, master, moment_one, moment_two):
    whole_acts = lax.all_gather(acts, "col", axis=0, tiled=True)
    tokens_total = acts.shape[0] * lax.axis_size("col") * lax.axis_size("depth")
    whole_cotangent = lax.all_gather(grad_out, "row", axis=0, tiled=True)
    picked = whole_cotangent
    input_sum = lax.psum_scatter(
        lax.dot_general(
            picked, weight, (((1,), (1,)), ((), ())), preferred_element_type=jnp.float32
        ),
        "col",
        scatter_dimension=0,
        tiled=True,
    )
    picked = whole_acts
    grad_sum = lax.psum_scatter(
        lax.dot_general(
            picked, whole_cotangent, (((0,), (0,)), ((), ())), preferred_element_type=jnp.float32
        ).astype(jnp.bfloat16),
        "depth",
        scatter_dimension=0,
        tiled=True,
    ).astype(jnp.float32)
    grad_in = input_sum.astype(jnp.bfloat16)
    grad = grad_sum * jnp.float32(1.0 / math.sqrt(tokens_total))
    new_moment_one = 0.9 * moment_one + 0.1 * grad
    new_moment_two = 0.95 * moment_two + 0.05 * grad * grad
    first_fix = 1.0 - 0.9**STEP
    second_fix = 1.0 - 0.95**STEP
    update = new_moment_one / first_fix / (jnp.sqrt(new_moment_two / second_fix) + 1e-08)
    new_master = master - 0.01 * (update + 0.1 * master)
    new_weight = lax.all_gather(new_master.astype(jnp.bfloat16), "depth", axis=0, tiled=True)
    return (grad_in, new_weight, new_master, new_moment_one, new_moment_two)


def solution(mesh):
    placed = (
        P(("depth", "col"), "row"),
        P(("depth", "row"), "col"),
        P("row", "col"),
        P(("row", "depth"), "col"),
        P(("row", "depth"), "col"),
        P(("row", "depth"), "col"),
    )
    return jax.shard_map(
        per_device,
        mesh=mesh,
        in_specs=placed,
        out_specs=(
            P(("depth", "col"), "row"),
            P("row", "col"),
            P(("row", "depth"), "col"),
            P(("row", "depth"), "col"),
            P(("row", "depth"), "col"),
        ),
        check_vma=False,
    )
```

profile of v0, /device:TPU:0, one launch (start us, length us, event | category | flops | bytes accessed | tf_op | source)
XLA Modules:
  0.0 1031.1 jit_solution(5081694535935332860)
XLA Ops:
  7.2 0.0 all-gather.4.cloned.1.call-start
  7.2 0.7 all-gather.4.cloned.1.call-update
  7.9 0.0 all-gather.6.cloned.1.call-start
  7.9 0.7 all-gather.6.cloned.1.call-update
  8.6 0.0 reduce-scatter.5.cloned.1.call-start
  8.7 173.3 %all-gather.4.cloned.1.call-done = bf16[2048,3456]{1,0:T(8,128)(2,1)} async-done(((bf16[1024,3456]{1,0:T(8,128)(2,1)}), bf16[2048,3456]{1,0:T(8,128)(2,1)}) %all-gather.4.cloned.1.call-update) | async-done | bytes 14155792 | tf_op jit(solution)/shard_map/all_gather | solution.py:13
  182.0 185.5 %all-gather.6.cloned.1.call-done = bf16[2048,2560]{1,0:T(8,128)(2,1)} async-done(((bf16[512,2560]{1,0:T(8,128)(2,1)}), bf16[2048,2560]{1,0:T(8,128)(2,1)}) %all-gather.6.cloned.1.call-update) | async-done | bytes 10485776 | tf_op jit(solution)/shard_map/all_gather | solution.py:11
  367.5 45.6 %convolution_convert_fusion = bf16[2560,3456]{1,0:T(8,128)(2,1)} fusion(bf16[2048,2560]{1,0:T(8,128)(2,1)} %all-gather.6.cloned.1.call-done, bf16[2048,3456]{1,0:T(8,128)(2,1)} %all-gather.4.cloned.1.call-done), kind=kOutput, calls=%fused_computation | convolution fusion | flops 36247633920 | bytes 42336256 | tf_op jit(solution)/shard_map/dot_general | solution.py:25
  413.1 0.0 reduce-scatter.5.cloned.1.call-update
  413.2 0.0 reduce-scatter.3.cloned.1.call-start
  413.2 47.3 %fusion.6 = f32[2048,2560]{1,0:T(8,128)} fusion(bf16[2048,3456]{1,0:T(8,128)(2,1)} %all-gather.4.cloned.1.call-done, bf16[2560,3456]{1,0:T(8,128)(2,1)} %param.8), kind=kOutput, calls=%fused_computation.9 | convolution fusion | flops 36238786560 | bytes 52822016 | tf_op jit(solution)/shard_map/dot_general | solution.py:16
  460.5 0.0 reduce-scatter.3.cloned.1.call-update
  460.5 0.2 all-gather.8.cloned.1.call-start
  460.8 81.3 %reduce-scatter.5.cloned.1.call-done = bf16[640,3456]{1,0:T(8,128)(2,1)} async-done(((bf16[2560,3456]{1,0:T(8,128)(2,1)}), bf16[640,3456]{1,0:T(8,128)(2,1)}) %reduce-scatter.5.cloned.1.call-update) | async-done | bytes 4423696 | tf_op jit(solution)/shard_map/reduce_scatter | solution.py:24
  542.1 23.0 %fusion.3 = (bf16[640,3456]{1,0:T(8,128)(2,1)}, f32[640,3456]{1,0:T(8,128)}, f32[640,3456]{1,0:T(8,128)}, f32[640,3456]{1,0:T(8,128)}) fusion(f32[640,3456]{1,0:T(8,128)} %param.9, bf16[640,3456]{1,0:T(8,128)(2,1)} %reduce-scatter.5.cloned.1.call-done, f32[640,3456]{1,0:T(8,128)} %param.10, f32[640,3456]{1,0:T(8,128)} %param.11), kind=kLoop, calls=%fused_computation.8 | loop fusion | flops 39813120 | bytes 61931520 | tf_op jit(solution)/shard_map/convert_element_type | solution.py:40
  565.1 0.0 all-gather.8.cloned.1.call-update
  565.2 326.6 %reduce-scatter.3.cloned.1.call-done = f32[512,2560]{1,0:T(8,128)} async-done(((f32[2048,2560]{1,0:T(8,128)}), f32[512,2560]{1,0:T(8,128)}) %reduce-scatter.3.cloned.1.call-update) | async-done | bytes 5242896 | tf_op jit(solution)/shard_map/reduce_scatter | solution.py:15
  891.7 4.3 convert_element_type.12
  896.0 112.6 %all-gather.8.cloned.1.call-done = bf16[2560,3456]{1,0:T(8,128)(2,1)} async-done(((bf16[640,3456]{1,0:T(8,128)(2,1)}), bf16[2560,3456]{1,0:T(8,128)(2,1)}) %all-gather.8.cloned.1.call-update) | async-done | bytes 17694736 | tf_op jit(solution)/shard_map/all_gather | solution.py:40
  1008.6 16.0 %copy.12 = bf16[2560,3456]{1,0:T(8,128)(2,1)} copy(bf16[2560,3456]{1,0:T(8,128)(2,1)} %all-gather.8.cloned.1.call-done) | data formatting | bytes 35389440
Async XLA Ops:
  7.2 174.9 %all-gather.4.cloned.1.call-start = ((), (), s32[]{:S(2)}) async-start(), calls=%async_computation.2 | async-start | bytes 21233664 | tf_op jit(solution)/shard_map/all_gather | solution.py:13
  7.9 359.6 %all-gather.6.cloned.1.call-start = ((), (), s32[]{:S(2)}) async-start(), calls=%async_computation.4 | async-start | bytes 13107200 | tf_op jit(solution)/shard_map/all_gather | solution.py:11
  8.6 533.5 %reduce-scatter.5.cloned.1.call-start = ((), (), s32[]{:S(2)}) async-start(), calls=%async_computation.5 | async-start | bytes 22118400 | tf_op jit(solution)/shard_map/reduce_scatter | solution.py:24
  413.2 478.6 %reduce-scatter.3.cloned.1.call-start = ((), (), s32[]{:S(2)}) async-start(), calls=%async_computation.3 | async-start | bytes 26214400 | tf_op jit(solution)/shard_map/reduce_scatter | solution.py:15
  460.5 548.0 %all-gather.8.cloned.1.call-start = ((), (), s32[]{:S(2)}) async-start(), calls=%async_computation.6 | async-start | bytes 22118400 | tf_op jit(solution)/shard_map/all_gather | solution.py:40
Sparse Core Ops, SparseCore 0:
  9.5 172.4 all-gather.3
  183.6 183.8 all-gather.5
  413.3 128.7 reduce-scatter.4
  544.3 347.3 reduce-scatter.2
  893.7 114.7 all-gather.7
where the time goes:
time: 1030 us
  waiting for transfers between devices  881 us (86%)
  matrix products  92.9 us (9%)
  other arithmetic  27.3 us (3%)
  local copies, waits for them, and re-layouts  16 us (2%)
  between operations  13.8 us (1%)
    reduce_scatter x1, waiting for transfers between devices, per_device(): lax.psum_scatter(lax.dot_general(picked, weight, (((1,), (1,)), ((), ()))...  327 us
    all_gather x1, waiting for transfers between devices, per_device(): whole_acts = lax.all_gather(acts, 'col', axis=0, tiled=True)  185 us
    all_gather x1, waiting for transfers between devices, per_device(): whole_cotangent = lax.all_gather(grad_out, 'row', axis=0, tiled=True)  173 us
    all_gather x1, waiting for transfers between devices, per_device(): lax.all_gather(new_master.astype(jnp.bfloat16), 'depth', axis=0, tiled=True)  113 us
    reduce_scatter x1, waiting for transfers between devices, per_device(): lax.psum_scatter(lax.dot_general(picked, whole_cotangent, (((0,), (0,)),...  81.3 us
    dot_general x1, matrix products, per_device(): lax.dot_general(picked, weight, (((1,), (1,)), ((), ())), preferred_eleme...  47.3 us
    dot_general x1, matrix products, per_device(): lax.dot_general(picked, whole_cotangent, (((0,), (0,)), ((), ())), prefer...  45.6 us
    convert_element_type x1, other arithmetic, per_device(): new_master.astype(jnp.bfloat16)  23 us
  transfers between devices with their start and end apart: 5, of which 5 were waited for; matrix products, arithmetic and copies ran while one was open for 7% of the time, Pallas kernels for 0%

commit v1 on v0

--- a/solution.py
+++ b/solution.py
@@ -3,12 +3,26 @@
 import jax.numpy as jnp
 from jax import lax
 from jax.sharding import PartitionSpec as P
+from jax.lax import axis_index, axis_size, ppermute
 
 STEP = 10
 
 
 def per_device(acts, grad_out, weight, master, moment_one, moment_two):
-    whole_acts = lax.all_gather(acts, "col", axis=0, tiled=True)
+
+    def flows_post(local_block, which_axis):
+        count_all = axis_size(which_axis)
+        pages = [(ix, (ix + 1) % count_all) for ix in range(count_all)]
+
+        def read_lane(after):
+            if len(after) == count_all:
+                return after
+            return read_lane([ppermute(after[0], which_axis, pages), *after])
+
+        y2 = jnp.concatenate(read_lane([local_block]), axis=0)
+        return jnp.roll(y2, shift=(axis_index(which_axis) + 1) * local_block.shape[0], axis=0)
+
+    whole_acts = flows_post(acts, "col")
     tokens_total = acts.shape[0] * lax.axis_size("col") * lax.axis_size("depth")
     whole_cotangent = lax.all_gather(grad_out, "row", axis=0, tiled=True)
     picked = whole_cotangent

time: 1030 us -> 875 us (0.85)
  waiting for transfers between devices: 881 us -> 699 us
  local copies, waits for them, and re-layouts: 16 us -> 37.8 us
    all_gather x1 -> x0, waiting for transfers between devices: 185 us -> none  [per_device(): whole_acts = lax.all_gather(acts, 'col', axis=0, tiled=True)]
    ppermute x0 -> x3, waiting for transfers between devices: none -> 178 us  [read_lane(): return read_lane([ppermute(after[0], which_axis, pages), *after])]
    all_gather x1, waiting for transfers between devices: 173 us -> 0.01 us  [per_device(): whole_cotangent = lax.all_gather(grad_out, 'row', axis=0, tiled=True)]
    unnamed x1 -> x14, local copies, waits for them, and re-layouts: 16 us -> 36.2 us
  transfers between devices with their start and end apart: 5 -> 7, of which waited for: 5 -> 6; matrix products, arithmetic and copies ran while one was open for 7% -> 11% of each run, Pallas kernels for 0% -> 0%
where the time goes in v1:
time: 875 us; the launch traced here: 874 us
  waiting for transfers between devices  699 us (80%)
  matrix products  93.3 us (11%)
  local copies, waits for them, and re-layouts  37.8 us (4%)
  other arithmetic  27.3 us (3%)
  between operations  13.8 us (2%)
    reduce_scatter x1, waiting for transfers between devices, per_device(): lax.psum_scatter(lax.dot_general(picked, weight, (((1,), (1,)), ((), ()))...  327 us
    ppermute x3, waiting for transfers between devices, read_lane(): return read_lane([ppermute(after[0], which_axis, pages), *after])  178 us
    all_gather x1, waiting for transfers between devices, per_device(): lax.all_gather(new_master.astype(jnp.bfloat16), 'depth', axis=0, tiled=True)  113 us
    reduce_scatter x1, waiting for transfers between devices, per_device(): lax.psum_scatter(lax.dot_general(picked, whole_cotangent, (((0,), (0,)),...  80.6 us
    dot_general x1, matrix products, per_device(): lax.dot_general(picked, weight, (((1,), (1,)), ((), ())), preferred_eleme...  47.7 us
    dot_general x1, matrix products, per_device(): lax.dot_general(picked, whole_cotangent, (((0,), (0,)), ((), ())), prefer...  45.6 us
    unnamed x14, local copies, waits for them, and re-layouts  36.2 us
    convert_element_type x1, other arithmetic, per_device(): new_master.astype(jnp.bfloat16)  23 us
  transfers between devices with their start and end apart: 7, of which 6 were waited for; matrix products, arithmetic and copies ran while one was open for 11% of the time, Pallas kernels for 0%

profile of v1, /device:TPU:0, one launch (start us, length us, event | category | flops | bytes accessed | tf_op | source)
XLA Modules:
  0.0 874.5 jit_solution(2497465985580016966)
XLA Ops:
  7.2 0.0 all-gather.3.cloned.1.call-start
  7.2 0.7 all-gather.3.cloned.1.call-update
  7.9 0.0 copy-start
  7.9 0.0 reduce-scatter.5.cloned.1.call-start
  8.0 3.1 collective-permute-start
  11.1 59.1 %collective-permute-done = bf16[512,2560]{1,0:T(8,128)(2,1)S(1)} collective-permute-done((bf16[512,2560]{1,0:T(8,128)(2,1)}, bf16[512,2560]{1,0:T(8,128)(2,1)S(1)}, u32[]{:S(2)}, u32[]{:S(2)}) %collective-permute-start) | collective-permute-done | bytes 2621472 | tf_op jit(solution)/shard_map/ppermute | solution.py:20
  70.2 0.0 copy-start.1
  70.2 1.5 copy-done.1
  71.7 0.0 collective-permute-start.1
  71.7 59.9 %collective-permute-done.1 = bf16[512,2560]{1,0:T(8,128)(2,1)} collective-permute-done((bf16[512,2560]{1,0:T(8,128)(2,1)S(1)}, bf16[512,2560]{1,0:T(8,128)(2,1)}, u32[]{:S(2)}, u32[]{:S(2)}) %collective-permute-start.1) | collective-permute-done | bytes 2621472 | tf_op jit(solution)/shard_map/ppermute | solution.py:20
  131.6 0.0 collective-permute-start.2
  131.6 0.0 copy-start.2
  131.6 59.3 %collective-permute-done.2 = bf16[512,2560]{1,0:T(8,128)(2,1)} collective-permute-done((bf16[512,2560]{1,0:T(8,128)(2,1)}, bf16[512,2560]{1,0:T(8,128)(2,1)}, u32[]{:S(2)}, u32[]{:S(2)}) %collective-permute-start.2) | collective-permute-done | bytes 2621472 | tf_op jit(solution)/shard_map/ppermute | solution.py:20
  190.9 3.4 constant_dynamic-update-slice_fusion.7
  194.3 3.4 constant_dynamic-update-slice_fusion.6
  197.7 0.0 copy-done.2
  197.7 1.6 constant_dynamic-update-slice_fusion.5
  199.4 0.0 copy-done
  199.4 1.7 constant_dynamic-update-slice_fusion.4
  201.1 3.5 constant_dynamic-update-slice_fusion.3
  204.5 3.4 constant_dynamic-update-slice_fusion.2
  207.9 1.7 constant_dynamic-update-slice_fusion.1
  209.6 1.6 constant_dynamic-update-slice_fusion
  211.2 0.0 all-gather.3.cloned.1.call-done
  211.2 45.6 %convolution_convert_fusion = bf16[2560,3456]{1,0:T(8,128)(2,1)} fusion(bf16[2048,3456]{1,0:T(8,128)(2,1)} %all-gather.3.cloned.1.call-done, bf16[4096,2560]{1,0:T(8,128)(2,1)} %constant_dynamic-update-slice_fusion, s32[]{:T(128)S(6)} %select_n.14), kind=kOutput, calls=%fused_computation | convolution fusion | flops 36247633920 | bytes 42336260 | tf_op jit(solution)/shard_map/dot_general | solution.py:39
  256.8 0.0 reduce-scatter.5.cloned.1.call-update
  256.8 0.0 reduce-scatter.3.cloned.1.call-start
  256.9 47.7 %fusion.8 = f32[2048,2560]{1,0:T(8,128)} fusion(bf16[2048,3456]{1,0:T(8,128)(2,1)} %all-gather.3.cloned.1.call-done, bf16[2560,3456]{1,0:T(8,128)(2,1)} %param.8), kind=kOutput, calls=%fused_computation.19 | convolution fusion | flops 36238786560 | bytes 52822016 | tf_op jit(solution)/shard_map/dot_general | solution.py:30
  304.6 0.0 reduce-scatter.3.cloned.1.call-update
  304.6 0.2 all-gather.5.cloned.1.call-start
  304.8 80.6 %reduce-scatter.5.cloned.1.call-done = bf16[640,3456]{1,0:T(8,128)(2,1)} async-done(((bf16[2560,3456]{1,0:T(8,128)(2,1)}), bf16[640,3456]{1,0:T(8,128)(2,1)}) %reduce-scatter.5.cloned.1.call-update) | async-done | bytes 4423696 | tf_op jit(solution)/shard_map/reduce_scatter | solution.py:38
  385.4 23.0 %fusion.5 = (bf16[640,3456]{1,0:T(8,128)(2,1)}, f32[640,3456]{1,0:T(8,128)}, f32[640,3456]{1,0:T(8,128)}, f32[640,3456]{1,0:T(8,128)}) fusion(f32[640,3456]{1,0:T(8,128)} %param.9, bf16[640,3456]{1,0:T(8,128)(2,1)} %reduce-scatter.5.cloned.1.call-done, f32[640,3456]{1,0:T(8,128)} %param.10, f32[640,3456]{1,0:T(8,128)} %param.11), kind=kLoop, calls=%fused_computation.18 | loop fusion | flops 39813120 | bytes 61931520 | tf_op jit(solution)/shard_map/convert_element_type | solution.py:54
  408.4 0.0 all-gather.5.cloned.1.call-update
  408.4 326.7 %reduce-scatter.3.cloned.1.call-done = f32[512,2560]{1,0:T(8,128)} async-done(((f32[2048,2560]{1,0:T(8,128)}), f32[512,2560]{1,0:T(8,128)}) %reduce-scatter.3.cloned.1.call-update) | async-done | bytes 5242896 | tf_op jit(solution)/shard_map/reduce_scatter | solution.py:29
  735.1 4.3 convert_element_type.12
  739.4 112.5 %all-gather.5.cloned.1.call-done = bf16[2560,3456]{1,0:T(8,128)(2,1)} async-done(((bf16[640,3456]{1,0:T(8,128)(2,1)}), bf16[2560,3456]{1,0:T(8,128)(2,1)}) %all-gather.5.cloned.1.call-update) | async-done | bytes 17694736 | tf_op jit(solution)/shard_map/all_gather | solution.py:54
  851.9 16.0 %copy.19 = bf16[2560,3456]{1,0:T(8,128)(2,1)} copy(bf16[2560,3456]{1,0:T(8,128)(2,1)} %all-gather.5.cloned.1.call-done) | data formatting | bytes 35389440
Async XLA Ops:
  7.2 204.0 %all-gather.3.cloned.1.call-start = ((), (), s32[]{:S(2)}) async-start(), calls=%async_computation.2 | async-start | bytes 21233664 | tf_op jit(solution)/shard_map/all_gather | solution.py:27
  7.9 191.5 %copy-start = (bf16[512,2560]{1,0:T(8,128)(2,1)S(1)}, bf16[512,2560]{1,0:T(8,128)(2,1)}, u32[]{:S(2)}) copy-start(bf16[512,2560]{1,0:T(8,128)(2,1)} %param.6) | copy-start | bytes 7864324
  7.9 377.5 %reduce-scatter.5.cloned.1.call-start = ((), (), s32[]{:S(2)}) async-start(), calls=%async_computation.4 | async-start | bytes 22118400 | tf_op jit(solution)/shard_map/reduce_scatter | solution.py:38
  8.0 62.2 %collective-permute-start = (bf16[512,2560]{1,0:T(8,128)(2,1)}, bf16[512,2560]{1,0:T(8,128)(2,1)S(1)}, u32[]{:S(2)}, u32[]{:S(2)}) collective-permute-start(bf16[512,2560]{1,0:T(8,128)(2,1)} %param.6), channel_id=1, source_target_pairs={{0,4},{4,8},{8,12},{12,0},{1,5},{5,9},{9,13},{13,1},{2,6},{6,10},{... | collective-permute-start | bytes 7864328 | tf_op jit(solution)/shard_map/ppermute | solution.py:20
  70.2 1.5 copy-start.1
  71.7 59.9 %collective-permute-start.1 = (bf16[512,2560]{1,0:T(8,128)(2,1)S(1)}, bf16[512,2560]{1,0:T(8,128)(2,1)}, u32[]{:S(2)}, u32[]{:S(2)}) collective-permute-start(bf16[512,2560]{1,0:T(8,128)(2,1)S(1)} %collective-permute-done), channel_id=1, source_target_pairs={{0,4},{4,8},{8,12},{12,0},{1,5},{5,9},{9,13},{13,1},{2,6},{6,10},{... | collective-permute-start | bytes 7864328 | tf_op jit(solution)/shard_map/ppermute | solution.py:20
  131.6 59.3 %collective-permute-start.2 = (bf16[512,2560]{1,0:T(8,128)(2,1)}, bf16[512,2560]{1,0:T(8,128)(2,1)}, u32[]{:S(2)}, u32[]{:S(2)}) collective-permute-start(bf16[512,2560]{1,0:T(8,128)(2,1)} %collective-permute-done.1), channel_id=1, source_target_pairs={{0,4},{4,8},{8,12},{12,0},{1,5},{5,9},{9,13},{13,1},{2,6},{6,10},{... | collective-permute-start | bytes 7864328 | tf_op jit(solution)/shard_map/ppermute | solution.py:20
  131.6 66.1 %copy-start.2 = (bf16[512,2560]{1,0:T(8,128)(2,1)S(1)}, bf16[512,2560]{1,0:T(8,128)(2,1)}, u32[]{:S(2)}) copy-start(bf16[512,2560]{1,0:T(8,128)(2,1)} %copy-done.1) | copy-start | bytes 7864324
  256.8 478.3 %reduce-scatter.3.cloned.1.call-start = ((), (), s32[]{:S(2)}) async-start(), calls=%async_computation.3 | async-start | bytes 26214400 | tf_op jit(solution)/shard_map/reduce_scatter | solution.py:29
  304.6 547.4 %all-gather.5.cloned.1.call-start = ((), (), s32[]{:S(2)}) async-start(), calls=%async_computation.5 | async-start | bytes 22118400 | tf_op jit(solution)/shard_map/all_gather | solution.py:54
Sparse Core Ops, SparseCore 0:
  9.5 172.4 all-gather.2
  257.0 128.3 reduce-scatter.4
  387.7 347.3 reduce-scatter.2
  737.1 114.7 all-gather.4
